TPU v7x, 32 devices: a whole 2x2x4 slice. The times are simulated.
32 devices in a mesh: scen: 8 (over y, x, core), col: 4 (over z).
Axes of the slice: x: 2, y: 2, z: 4, core: 2. Of those that a mesh axis runs over, the one named last changes fastest.
Arguments:
- coef: float32 [4096, 8192], P('scen', 'col'), as said below
- mask: int32 [4096], replicated, may hold values from 0 to 1, as said below
- assign: int32 [512], replicated, may hold values from 0 to 511, each once
Outputs:
- master: float32 [4, 2048, 4096], P('col', 'scen')
Inputs may be any that keep to these rules, and one draw needn't show every extreme that they name: `mask`: in each aligned block of 512 cuts (the cuts of one index of scen) exactly 256 are active. `coef`: magnitudes of rows and of columns differ widely; entries are finite and not zero on every row.
All inputs are finite; a program needn't handle non-finite values.
Results may differ from a plain program's by a relative error of at most 0.00007.
Values sent between devices are 32-bit elements; how exact they have to be, the bound alone decides.
No kernel may reach another device: no remote copies, remote signals or barrier semaphores. Data moves between devices by JAX's collectives and lax.ppermute only.
A program may use at most 128 MiB of HBM per device.

v0:
```python
import jax
import jax.numpy as jnp
from jax import lax
from jax.sharding import PartitionSpec as P

NV = 8192
K = 8
ACT_DEV = 256
EPS = 1e-06


def on_device(coef, mask, assign):
    rows, width = coef.shape
    groups = lax.axis_size("scen")
    slice_width = width // groups
    cut_total = groups * rows
    slot_total = cut_total // K
    active_total = ACT_DEV * groups
    partial_value = jnp.sum(coef * coef, axis=1)
    total = lax.psum(partial_value, "col")
    row_norm = jnp.sqrt(total / NV + EPS)
    device_index = lax.axis_index("scen")
    own_mask = lax.dynamic_slice_in_dim(mask, device_index * rows, rows)
    live = own_mask.astype(jnp.float32)
    scaled = coef / row_norm[:, None] * live[:, None]
    flipped = scaled.T.reshape(groups, slice_width, rows)
    inverse = jnp.argsort(assign, stable=True)
    kept_rows = jnp.argsort(1 - own_mask, stable=True)[:ACT_DEV]
    picked = jnp.take(flipped, kept_rows, axis=2)
    arrived = lax.all_to_all(picked, "scen", split_axis=0, concat_axis=2, tiled=True)
    norm = jnp.sqrt(jnp.sum(arrived * arrived, axis=2, keepdims=True) / active_total + EPS)
    equil = (arrived / norm).reshape(slice_width, groups, ACT_DEV)
    block_masks = mask.reshape(groups, rows)
    chosen = jnp.argsort(1 - block_masks, axis=1, stable=True)[:, :ACT_DEV]
    bundle = min(groups, 8)
    rounds = groups // bundle
    chosen_sets = chosen.reshape(rounds, bundle, ACT_DEV)
    equil_sets = equil.reshape(slice_width, rounds, bundle, ACT_DEV).transpose(1, 0, 2, 3)
    local_rows = jnp.arange(rows, dtype=jnp.int32)

    def place(pair):
        chosen_set, equil_set = pair
        placing = (chosen_set[:, :, None] == local_rows[None, None, :]).astype(jnp.float32)
        return jnp.einsum("sga,gar->sgr", equil_set, placing, precision=lax.Precision.HIGHEST)

    placed = lax.map(place, (chosen_sets, equil_sets))
    whole = placed.transpose(1, 0, 2, 3).reshape(1, slice_width, cut_total)
    slotted = whole.reshape(1, slice_width, slot_total, K)
    return jnp.take(slotted, inverse, axis=2).reshape(1, slice_width, cut_total)


def solution(mesh):
    in_specs = (P("scen", "col"), P(), P())
    out_specs = P("col", "scen", None)
    return jax.shard_map(
        on_device, mesh=mesh, in_specs=in_specs, out_specs=out_specs, check_vma=False
    )
```

profile of v0, /device:TPU:0, one launch (start us, length us, event | category | flops | bytes accessed | tf_op | source)
XLA Modules:
  0.0 95.5 jit_solution(2898095278292690837)
XLA Ops:
  6.5 0.8 dynamic-slice_subtract_fusion
  7.3 3.8 %sort.50 = (s32[512]{0:T(512)}, s32[512]{0:T(512)S(1)}) sort(s32[512]{0:T(512)S(1)} %get-tuple-element.26, s32[512]{0:T(512)S(1)} %iota.20), dimensions={0}, to_apply=%region_2.0 | sort | flops 4608 | bytes 8192 | tf_op jit(solution)/shard_map/jit(argsort)/sort | solution.py:28
  11.1 2.5 %multiply_reduce_fusion = f32[512]{0:T(512)S(1)} fusion(f32[512,2048]{1,0:T(8,128)} %param.3), kind=kLoop, calls=%fused_computation.4 | loop fusion | flops 2096640 | bytes 4196352 | tf_op jit(solution)/shard_map/reduce_sum | solution.py:19
  13.6 13.5 %psum.7 = f32[512]{0:T(512)S(1)} all-reduce(f32[512]{0:T(512)S(1)} %multiply_reduce_fusion), channel_id=1, replica_groups=mesh['scen'=8,'col'=4] {'col'}, use_global_device_ids=true, to_apply=%region_4.5 | all-reduce | flops 512 | bytes 4096 | tf_op jit(solution)/shard_map/psum | solution.py:20
  27.1 2.6 %divide_multiply_fusion = f32[512,2048]{1,0:T(8,128)S(1)} fusion(f32[512,2048]{1,0:T(8,128)} %param.3, f32[512]{0:T(512)S(1)} %get-tuple-element.27, f32[512]{0:T(512)S(1)} %add_sqrt_fusion), kind=kLoop, calls=%fused_computation.3 | loop fusion | flops 2097152 | bytes 8392704 | tf_op jit(solution)/shard_map/mul | solution.py:25
  29.7 4.0 %copy.11 = f32[64,8,8,256]{3,2,1,0:T(8,128)} copy(f32[64,8,8,256]{3,1,2,0:T(8,128)S(1)} %bitcast.25) | data formatting | bytes 8388608
  33.7 2.9 %gather_fusion = f32[256,8,256]{2,1,0:T(8,128)S(1)} fusion(f32[8,256,512]{1,0,2:T(8,128)} %bitcast.26, s32[1024]{0:T(1024)S(1)} %pad_clamp_fusion.1), kind=kCustom, calls=%fused_computation | custom fusion | bytes 4195328 | tf_op jit(solution)/shard_map/jit(_take)/gather | solution.py:29
  36.6 0.3 select_bitcast_fusion
  37.0 2.0 %copy.7 = f32[8,256,256]{1,2,0:T(8,128)} copy(f32[8,256,256]{1,0,2:T(8,128)S(1)} %select_bitcast_fusion) | data formatting | bytes 4194304 | tf_op jit(solution)/shard_map/jit(_take)/select_n | solution.py:29
  39.0 3.7 %all-to-all-start = ((f32[8,256,256]{1,2,0:T(8,128)}), f32[8,256,256]{1,2,0:T(8,128)S(1)}, u32[]{:S(2)}, u32[]{:S(2)}) async-start(f32[8,256,256]{1,2,0:T(8,128)} %copy.7), calls=%async_computation | async-start | bytes 4194304 | tf_op jit(solution)/shard_map/all_to_all | solution.py:30
  42.7 0.0 sort.52.cloned.1.call-start
  42.8 0.6 sub.17
  43.4 0.6 iota.19
  44.0 3.8 %sort.48 = (s32[512]{0:T(512)}, s32[512]{0:T(512)S(1)}) sort(s32[512]{0:T(512)S(1)} %copy-done.1, s32[512]{0:T(512)S(1)} %iota.18), dimensions={0}, to_apply=%region_0.0 | sort | flops 4608 | bytes 8192 | tf_op jit(solution)/shard_map/jit(argsort)/sort | solution.py:27
  47.8 0.1 broadcast_in_dim.39
  47.9 0.2 broadcast_in_dim.40
  48.1 0.5 sort.52.cloned.1.call-done
  48.6 0.7 slice.6
  49.3 20.0 %all-to-all-done = f32[8,256,256]{1,2,0:T(8,128)S(1)} async-done(((f32[8,256,256]{1,2,0:T(8,128)}), f32[8,256,256]{1,2,0:T(8,128)S(1)}, u32[]{:S(2)}, u32[]{:S(2)}) %all-to-all-start) | async-done | bytes 2097184 | tf_op jit(solution)/shard_map/all_to_all | solution.py:30
  69.3 0.3 fusion.1
  69.6 4.5 %fusion = f32[8,512,256]{2,1,0:T(8,128)} fusion(f32[8,256,256]{1,2,0:T(8,128)S(1)} %all-to-all-done, s32[8,256]{1,0:T(8,128)S(1)} %slice.6, f32[256]{0:T(256)S(1)} %add_sqrt_fusion.1), kind=kOutput, calls=%fused_computation.6 | convolution fusion | flops 3222798336 | bytes 6300672 | tf_op jit(solution)/shard_map/while/body/eval_jaxpr/sga,gar->sgr/dot_general | solution.py:44
  74.1 5.1 %gather_fusion.1 = f32[512,256,8]{1,2,0:T(8,128)} fusion(f32[256,512,8]{0,2,1:T(8,128)} %bitcast.24, s32[1024]{0:T(1024)S(1)} %pad_clamp_fusion), kind=kCustom, calls=%fused_computation.1 | custom fusion | bytes 8390656 | tf_op jit(solution)/shard_map/jit(_take)/gather | solution.py:49
  79.2 3.9 %bitcast_select_fusion = f32[1,256,4096]{1,2,0:T(8,128)} fusion(f32[512,256,8]{1,2,0:T(8,128)} %gather_fusion.1, pred[4096]{0:T(1024)(128)(4,1)S(1)} %broadcast_in_dim.40), kind=kLoop, calls=%fused_computation.2 | loop fusion | flops 1048576 | bytes 8392704 | tf_op jit(solution)/shard_map/jit(_take)/select_n | solution.py:49
  83.1 5.6 %copy.9 = f32[1,256,4096]{2,1,0:T(8,128)} copy(f32[1,256,4096]{1,2,0:T(8,128)} %bitcast_select_fusion) | data formatting | bytes 8388608 | tf_op jit(solution)/shard_map/jit(_take)/select_n | solution.py:49
  (16 shorter events, 0.1 us)
Async XLA Ops:
  37.0 5.8 %copy-start = (s32[4096]{0:T(1024)S(1)}, s32[4096]{0:T(1024)}, u32[]{:S(2)}) copy-start(s32[4096]{0:T(1024)} %param.4) | copy-start | bytes 49156
  37.0 7.0 %copy-start.1 = (s32[512]{0:T(512)S(1)}, s32[512]{0:T(512)}, u32[]{:S(2)}) copy-start(s32[512]{0:T(512)} %param.5) | copy-start | bytes 6148
  39.0 30.3 %all-to-all-start = ((f32[8,256,256]{1,2,0:T(8,128)}), f32[8,256,256]{1,2,0:T(8,128)S(1)}, u32[]{:S(2)}, u32[]{:S(2)}) async-start(f32[8,256,256]{1,2,0:T(8,128)} %copy.7), calls=%async_computation | async-start | bytes 4194304 | tf_op jit(solution)/shard_map/all_to_all | solution.py:30
  42.7 5.9 %sort.52.cloned.1.call-start = ((), (), s32[]{:S(2)}) async-start(), calls=%async_computation.1 | async-start | bytes 98336 | tf_op jit(solution)/shard_map/jit(argsort)/sort | solution.py:34
Sparse Core Ops, SparseCore 0:
  45.9 2.4 sort.54.cloned.1.call-done
  (1 shorter events, 0.0 us)
where the time goes:
time: 96.1 us; the launch traced here: 95.5 us
  local copies, waits for them, and re-layouts  22.3 us (23%)
  waiting for transfers between devices  20 us (21%)
  other arithmetic  18 us (19%)
  blocking collectives  13.5 us (14%)
  between operations  13.5 us (14%)
  matrix products  4.46 us (5%)
  starting transfers between devices  3.72 us (4%)
    all_to_all x1, waiting for transfers between devices, on_device(): lax.all_to_all(picked, 'scen', split_axis=0, concat_axis=2, tiled=True)  20 us
    psum x1, blocking collectives, on_device(): total = lax.psum(partial_value, 'col')  13.5 us
    select_n x1, local copies, waits for them, and re-layouts, on_device(): return jnp.take(slotted, inverse, axis=2).reshape(1, slice_width, cut_total)  5.59 us
    gather x1, local copies, waits for them, and re-layouts, on_device(): return jnp.take(slotted, inverse, axis=2).reshape(1, slice_width, cut_total)  5.08 us
    dot_general x1, matrix products, place(): jnp.einsum('sga,gar->sgr', equil_set, placing, precision=lax.Precision.HI...  4.46 us
    unnamed x6, local copies, waits for them, and re-layouts  4 us
    select_n x2, other arithmetic, on_device(): return jnp.take(slotted, inverse, axis=2).reshape(1, slice_width, cut_total)  3.91 us
    sort x1, other arithmetic, on_device(): kept_rows = jnp.argsort(1 - own_mask, stable=True)[:ACT_DEV]  3.77 us
  transfers between devices with their start and end apart: 1, of which 1 were waited for; matrix products, arithmetic and copies ran while one was open for 6% of the time, Pallas kernels for 0%

commit v1 on v0

--- a/solution.py
+++ b/solution.py
@@ -17,7 +17,9 @@
     slot_total = cut_total // K
     active_total = ACT_DEV * groups
     partial_value = jnp.sum(coef * coef, axis=1)
-    total = lax.psum(partial_value, "col")
+    total = partial_value
+    for hop in (1, 2):
+        total = total + lax.ppermute(total, "col", [(dev, dev ^ hop) for dev in range(4)])
     row_norm = jnp.sqrt(total / NV + EPS)
     device_index = lax.axis_index("scen")
     own_mask = lax.dynamic_slice_in_dim(mask, device_index * rows, rows)

time: 96.1 us -> 89.5 us (0.931)
  blocking collectives: 13.5 us -> 0 us
  starting transfers between devices: 3.72 us -> 9.49 us
  waiting for transfers between devices: 20 us -> 21.9 us
    psum x1 -> x0, blocking collectives: 13.5 us -> none  [on_device(): total = lax.psum(partial_value, 'col')]
    ppermute x0 -> x2, starting transfers between devices: none -> 5.77 us  [on_device(): lax.ppermute(total, 'col', [(dev, dev ^ hop) for dev in range(4)])]
    ppermute x0 -> x2, waiting for transfers between devices: none -> 1.89 us  [on_device(): lax.ppermute(total, 'col', [(dev, dev ^ hop) for dev in range(4)])]
  transfers between devices with their start and end apart: 1 -> 3, of which waited for: 1 -> 2; matrix products, arithmetic and copies ran while one was open for 6% -> 11% of each run, Pallas kernels for 0% -> 0%
where the time goes in v1:
time: 89.5 us; the launch traced here: 89 us
  local copies, waits for them, and re-layouts  22.3 us (25%)
  waiting for transfers between devices  21.9 us (24%)
  other arithmetic  17.3 us (19%)
  between operations  13.5 us (15%)
  starting transfers between devices  9.49 us (11%)
  matrix products  4.46 us (5%)
    all_to_all x1, waiting for transfers between devices, on_device(): lax.all_to_all(picked, 'scen', split_axis=0, concat_axis=2, tiled=True)  20 us
    ppermute x2, starting transfers between devices, on_device(): lax.ppermute(total, 'col', [(dev, dev ^ hop) for dev in range(4)])  5.77 us
    select_n x1, local copies, waits for them, and re-layouts, on_device(): return jnp.take(slotted, inverse, axis=2).reshape(1, slice_width, cut_total)  5.59 us
    gather x1, local copies, waits for them, and re-layouts, on_device(): return jnp.take(slotted, inverse, axis=2).reshape(1, slice_width, cut_total)  5.08 us
    dot_general x1, matrix products, place(): jnp.einsum('sga,gar->sgr', equil_set, placing, precision=lax.Precision.HI...  4.46 us
    unnamed x6, local copies, waits for them, and re-layouts  3.99 us
    select_n x2, other arithmetic, on_device(): return jnp.take(slotted, inverse, axis=2).reshape(1, slice_width, cut_total)  3.91 us
    sort x1, other arithmetic, on_device(): kept_rows = jnp.argsort(1 - own_mask, stable=True)[:ACT_DEV]  3.77 us
  transfers between devices with their start and end apart: 3, of which 2 were waited for; matrix products, arithmetic and copies ran while one was open for 11% of the time, Pallas kernels for 0%

profile of v1, /device:TPU:0, one launch (start us, length us, event | category | flops | bytes accessed | tf_op | source)
XLA Modules:
  0.0 89.0 jit_solution(12835754770434270107)
XLA Ops:
  6.5 2.5 %multiply_reduce_fusion = f32[512]{0:T(512)S(1)} fusion(f32[512,2048]{1,0:T(8,128)} %param.3), kind=kLoop, calls=%fused_computation.4 | loop fusion | flops 2096640 | bytes 4196352 | tf_op jit(solution)/shard_map/reduce_sum | solution.py:19
  9.1 3.1 %collective-permute-start = (f32[512]{0:T(512)S(1)}, f32[512]{0:T(512)S(1)}, u32[]{:S(2)}, u32[]{:S(2)}) collective-permute-start(f32[512]{0:T(512)S(1)} %multiply_reduce_fusion), channel_id=1, source_target_pairs={{0,1},{1,0},{2,3},{3,2},{4,5},{5,4},{6,7},{7,6},{8,9},{9,8},{10,11... | collective-permute-start | bytes 6152 | tf_op jit(solution)/shard_map/ppermute | solution.py:22
  12.3 3.8 %sort.50 = (s32[512]{0:T(512)}, s32[512]{0:T(512)S(1)}) sort(s32[512]{0:T(512)S(1)} %get-tuple-element.26, s32[512]{0:T(512)S(1)} %iota.20), dimensions={0}, to_apply=%region_2.3 | sort | flops 4608 | bytes 8192 | tf_op jit(solution)/shard_map/jit(argsort)/sort | solution.py:30
  16.1 2.7 %collective-permute-start.1 = (f32[512]{0:T(512)S(1)}, f32[512]{0:T(512)S(1)}, u32[]{:S(2)}, u32[]{:S(2)}) collective-permute-start(f32[512]{0:T(512)S(1)} %add.49), channel_id=1, source_target_pairs={{0,2},{1,3},{2,0},{3,1},{4,6},{5,7},{6,4},{7,5},{8,10},{9,11},{10,... | collective-permute-start | bytes 6152 | tf_op jit(solution)/shard_map/ppermute | solution.py:22
  18.7 1.9 %collective-permute-done.1 = f32[512]{0:T(512)S(1)} collective-permute-done((f32[512]{0:T(512)S(1)}, f32[512]{0:T(512)S(1)}, u32[]{:S(2)}, u32[]{:S(2)}) %collective-permute-start.1) | collective-permute-done | bytes 2080 | tf_op jit(solution)/shard_map/ppermute | solution.py:22
  20.6 2.6 %divide_multiply_fusion = f32[512,2048]{1,0:T(8,128)S(1)} fusion(f32[512,2048]{1,0:T(8,128)} %param.3, f32[512]{0:T(512)S(1)} %get-tuple-element.27, f32[512]{0:T(512)S(1)} %add_sqrt_fusion), kind=kLoop, calls=%fused_computation.3 | loop fusion | flops 2097152 | bytes 8392704 | tf_op jit(solution)/shard_map/mul | solution.py:27
  23.3 4.0 %copy.11 = f32[64,8,8,256]{3,2,1,0:T(8,128)} copy(f32[64,8,8,256]{3,1,2,0:T(8,128)S(1)} %bitcast.25) | data formatting | bytes 8388608
  27.2 2.9 %gather_fusion = f32[256,8,256]{2,1,0:T(8,128)S(1)} fusion(f32[8,256,512]{1,0,2:T(8,128)} %bitcast.26, s32[1024]{0:T(1024)S(1)} %pad_clamp_fusion.1), kind=kCustom, calls=%fused_computation | custom fusion | bytes 4195328 | tf_op jit(solution)/shard_map/jit(_take)/gather | solution.py:31
  30.2 0.3 select_bitcast_fusion
  30.5 2.0 %copy.7 = f32[8,256,256]{1,2,0:T(8,128)} copy(f32[8,256,256]{1,0,2:T(8,128)S(1)} %select_bitcast_fusion) | data formatting | bytes 4194304 | tf_op jit(solution)/shard_map/jit(_take)/select_n | solution.py:31
  32.5 3.7 %all-to-all-start = ((f32[8,256,256]{1,2,0:T(8,128)}), f32[8,256,256]{1,2,0:T(8,128)S(1)}, u32[]{:S(2)}, u32[]{:S(2)}) async-start(f32[8,256,256]{1,2,0:T(8,128)} %copy.7), calls=%async_computation | async-start | bytes 4194304 | tf_op jit(solution)/shard_map/all_to_all | solution.py:32
  36.3 0.6 sub.17
  36.9 0.6 iota.19
  37.5 3.8 %sort.48 = (s32[512]{0:T(512)}, s32[512]{0:T(512)S(1)}) sort(s32[512]{0:T(512)S(1)} %copy-done.1, s32[512]{0:T(512)S(1)} %iota.18), dimensions={0}, to_apply=%region_0.0 | sort | flops 4608 | bytes 8192 | tf_op jit(solution)/shard_map/jit(argsort)/sort | solution.py:29
  41.3 0.1 broadcast_in_dim.39
  41.4 0.2 broadcast_in_dim.40
  41.6 0.5 sort.52.cloned.1.call-done
  42.1 0.7 slice.6
  42.8 20.0 %all-to-all-done = f32[8,256,256]{1,2,0:T(8,128)S(1)} async-done(((f32[8,256,256]{1,2,0:T(8,128)}), f32[8,256,256]{1,2,0:T(8,128)S(1)}, u32[]{:S(2)}, u32[]{:S(2)}) %all-to-all-start) | async-done | bytes 2097184 | tf_op jit(solution)/shard_map/all_to_all | solution.py:32
  62.8 0.3 fusion.1
  63.1 4.5 %fusion = f32[8,512,256]{2,1,0:T(8,128)} fusion(f32[8,256,256]{1,2,0:T(8,128)S(1)} %all-to-all-done, s32[8,256]{1,0:T(8,128)S(1)} %slice.6, f32[256]{0:T(256)S(1)} %add_sqrt_fusion.1), kind=kOutput, calls=%fused_computation.6 | convolution fusion | flops 3222798336 | bytes 6300672 | tf_op jit(solution)/shard_map/while/body/eval_jaxpr/sga,gar->sgr/dot_general | solution.py:46
  67.6 5.1 %gather_fusion.1 = f32[512,256,8]{1,2,0:T(8,128)} fusion(f32[256,512,8]{0,2,1:T(8,128)} %bitcast.24, s32[1024]{0:T(1024)S(1)} %pad_clamp_fusion), kind=kCustom, calls=%fused_computation.1 | custom fusion | bytes 8390656 | tf_op jit(solution)/shard_map/jit(_take)/gather | solution.py:51
  72.7 3.9 %bitcast_select_fusion = f32[1,256,4096]{1,2,0:T(8,128)} fusion(f32[512,256,8]{1,2,0:T(8,128)} %gather_fusion.1, pred[4096]{0:T(1024)(128)(4,1)S(1)} %broadcast_in_dim.40), kind=kLoop, calls=%fused_computation.2 | loop fusion | flops 1048576 | bytes 8392704 | tf_op jit(solution)/shard_map/jit(_take)/select_n | solution.py:51
  76.6 5.6 %copy.9 = f32[1,256,4096]{2,1,0:T(8,128)} copy(f32[1,256,4096]{1,2,0:T(8,128)} %bitcast_select_fusion) | data formatting | bytes 8388608 | tf_op jit(solution)/shard_map/jit(_take)/select_n | solution.py:51
  (20 shorter events, 0.2 us)
Async XLA Ops:
  6.5 5.7 %copy-start = (s32[4096]{0:T(1024)S(1)}, s32[4096]{0:T(1024)}, u32[]{:S(2)}) copy-start(s32[4096]{0:T(1024)} %param.4) | copy-start | bytes 49156
  9.1 7.0 %collective-permute-start = (f32[512]{0:T(512)S(1)}, f32[512]{0:T(512)S(1)}, u32[]{:S(2)}, u32[]{:S(2)}) collective-permute-start(f32[512]{0:T(512)S(1)} %multiply_reduce_fusion), channel_id=1, source_target_pairs={{0,1},{1,0},{2,3},{3,2},{4,5},{5,4},{6,7},{7,6},{8,9},{9,8},{10,11... | collective-permute-start | bytes 6152 | tf_op jit(solution)/shard_map/ppermute | solution.py:22
  16.1 4.5 %collective-permute-start.1 = (f32[512]{0:T(512)S(1)}, f32[512]{0:T(512)S(1)}, u32[]{:S(2)}, u32[]{:S(2)}) collective-permute-start(f32[512]{0:T(512)S(1)} %add.49), channel_id=1, source_target_pairs={{0,2},{1,3},{2,0},{3,1},{4,6},{5,7},{6,4},{7,5},{8,10},{9,11},{10,... | collective-permute-start | bytes 6152 | tf_op jit(solution)/shard_map/ppermute | solution.py:22
  30.5 7.0 %copy-start.1 = (s32[512]{0:T(512)S(1)}, s32[512]{0:T(512)}, u32[]{:S(2)}) copy-start(s32[512]{0:T(512)} %param.5) | copy-start | bytes 6148
  32.5 30.3 %all-to-all-start = ((f32[8,256,256]{1,2,0:T(8,128)}), f32[8,256,256]{1,2,0:T(8,128)S(1)}, u32[]{:S(2)}, u32[]{:S(2)}) async-start(f32[8,256,256]{1,2,0:T(8,128)} %copy.7), calls=%async_computation | async-start | bytes 4194304 | tf_op jit(solution)/shard_map/all_to_all | solution.py:32
  36.2 5.9 %sort.52.cloned.1.call-start = ((), (), s32[]{:S(2)}) async-start(), calls=%async_computation.1 | async-start | bytes 98336 | tf_op jit(solution)/shard_map/jit(argsort)/sort | solution.py:36
Sparse Core Ops, SparseCore 0:
  39.4 2.4 sort.54.cloned.1.call-done
  (1 shorter events, 0.0 us)
